TPU v7x, 32 devices: a whole 2x2x4 slice. The times are simulated.
32 devices in a mesh: rep: 8 (over y, x, core), shard: 4 (over z).
Axes of the slice: x: 2, y: 2, z: 4, core: 2. Of those that a mesh axis runs over, the one named last changes fastest.
Arguments:
- tokens: bfloat16 [32, 128, 1536], P(('rep', 'shard')), may hold values from -6 to 6
- cotangent: bfloat16 [32, 128, 1536], P(('rep', 'shard')), may hold values from -6 to 6
- lengths: int32 [32], replicated, may hold values from 1 to 128, 3072 in all
- deal_order: int32 [32], replicated, may hold values from 0 to 31, as said below
- attention_gain: bfloat16 [2, 1536], P(None, 'shard'), may hold values from 0.099609375 to 1.8984375
- query_weight: bfloat16 [2, 1536, 1536], P(None, 'shard'), may hold values from -0.15625 to 0.15625
- key_weight: bfloat16 [2, 1536, 768], P(None, 'shard'), may hold values from -0.15625 to 0.15625
- value_weight: bfloat16 [2, 1536, 768], P(None, 'shard'), may hold values from -0.15625 to 0.15625
- output_weight: bfloat16 [2, 1536, 1536], P(None, 'shard'), may hold values from -0.625 to 0.625
- feedforward_gain: bfloat16 [2, 1536], P(None, 'shard'), may hold values from 0.099609375 to 1.8984375
- gate_weight: bfloat16 [2, 1536, 4096], P(None, 'shard'), may hold values from -0.15625 to 0.15625
- up_weight: bfloat16 [2, 1536, 4096], P(None, 'shard'), may hold values from -0.15625 to 0.15625
- down_weight: bfloat16 [2, 4096, 1536], P(None, 'shard'), may hold values from -0.09375 to 0.09375
Outputs:
- layer_output: bfloat16 [32, 128, 1536], P(('rep', 'shard'))
- input_grad: bfloat16 [32, 128, 1536], P(('rep', 'shard'))
- attention_gain_grad: float32 [2, 1536], P(None, 'shard')
- query_weight_grad: float32 [2, 1536, 1536], P(None, 'shard')
- key_weight_grad: float32 [2, 1536, 768], P(None, 'shard')
- value_weight_grad: float32 [2, 1536, 768], P(None, 'shard')
- output_weight_grad: float32 [2, 1536, 1536], P(None, 'shard')
- feedforward_gain_grad: float32 [2, 1536], P(None, 'shard')
- gate_weight_grad: float32 [2, 1536, 4096], P(None, 'shard')
- up_weight_grad: float32 [2, 1536, 4096], P(None, 'shard')
- down_weight_grad: float32 [2, 4096, 1536], P(None, 'shard')
Inputs may be any that keep to these rules, and one draw needn't show every extreme that they name: deal_order is a permutation of the sequences with deal_order[j] % 4 == j % 4. `lengths`: the longest sequence fills all 128 slots.
All inputs are finite; a program needn't handle non-finite values.
Results may differ from a plain program's by a relative error of at most 0.028.
Values may be sent and summed in bfloat16 or wider, within the bound.
A program may use at most 448 MiB of HBM per device.

v0:
```python
import jax
import jax.numpy as jnp
from jax import lax
from jax.sharding import PartitionSpec as P

HEADS = 16
KV_HEADS = 8
HEAD = 96
LAYERS = 2


epsilon = 1e-05
rope_base = 100000.0
masked_score = -1e30


def rope_tables(row_count):
    position = jnp.arange(row_count).astype(jnp.float32)
    frequency = rope_base ** (-(2.0 * jnp.arange(HEAD // 2).astype(jnp.float32)) / HEAD)
    angles = position[:, None] * frequency[None, :]
    angles = jnp.concatenate([angles, angles], axis=1)
    return (jnp.cos(angles)[:, None, :], jnp.sin(angles)[:, None, :])


def rotate(vector, cosine, sine):
    halfway = vector.shape[-1] // 2
    turned = jnp.concatenate([-vector[..., halfway:], vector[..., :halfway]], axis=-1)
    return vector * cosine + turned * sine


def unrotate(vector, cosine, sine):
    halfway = vector.shape[-1] // 2
    scaled = vector * sine
    turned = jnp.concatenate([scaled[..., halfway:], -scaled[..., :halfway]], axis=-1)
    return vector * cosine + turned


def rms_scale(stream):
    return lax.rsqrt(jnp.mean(stream * stream, axis=-1, keepdims=True) + epsilon)


def left_product(left, right):
    return jnp.dot(left, right, preferred_element_type=jnp.float32)


def right_transposed(grad_rows, weight):
    return jnp.einsum("lf,df->ld", grad_rows, weight, preferred_element_type=jnp.float32)


def row_sum_product(inputs, grad_rows):
    return jnp.einsum("ld,lf->df", inputs, grad_rows, preferred_element_type=jnp.float32)


def norm_backward(normed_grad, stream, scale, gain):
    gain_grad = jnp.sum(normed_grad * stream * scale, axis=0)
    weighted = normed_grad * gain.astype(jnp.float32)
    stream_grad = scale * weighted - stream * (scale * scale * scale) * jnp.mean(
        weighted * stream, axis=-1, keepdims=True
    )
    return (gain_grad, stream_grad)


def pick_sequence(wanted, carry, piece):
    span_rows = piece.shape[0]
    inside = (wanted >= 0) & (wanted < span_rows)
    chosen = lax.dynamic_slice_in_dim(piece, jnp.clip(wanted, 0, span_rows - 1), 1, 0)
    return jnp.where(inside, chosen, carry)


def gather_forward(stacked, layer_index):
    return (
        lax.all_gather(stacked[0][layer_index], "shard", axis=0, tiled=True),
        lax.all_gather(stacked[1][layer_index], "shard", axis=0, tiled=True),
        lax.all_gather(stacked[2][layer_index], "shard", axis=0, tiled=True),
        lax.all_gather(stacked[3][layer_index], "shard", axis=0, tiled=True),
        lax.all_gather(stacked[4][layer_index], "shard", axis=0, tiled=True),
        lax.all_gather(stacked[5][layer_index], "shard", axis=0, tiled=True),
        lax.all_gather(stacked[6][layer_index], "shard", axis=0, tiled=True),
        lax.all_gather(stacked[7][layer_index], "shard", axis=0, tiled=True),
        lax.all_gather(stacked[8][layer_index], "shard", axis=0, tiled=True),
    )


def gather_backward(stacked, layer_index):
    return (
        lax.all_gather(stacked[0][layer_index], "shard", axis=0, tiled=True),
        lax.all_gather(stacked[1][layer_index], "shard", axis=0, tiled=True),
        lax.all_gather(stacked[2][layer_index], "shard", axis=0, tiled=True),
        lax.all_gather(stacked[3][layer_index], "shard", axis=0, tiled=True),
        lax.all_gather(stacked[4][layer_index], "shard", axis=0, tiled=True),
        lax.all_gather(stacked[5][layer_index], "shard", axis=0, tiled=True),
        lax.all_gather(stacked[6][layer_index], "shard", axis=0, tiled=True),
        lax.all_gather(stacked[7][layer_index], "shard", axis=0, tiled=True),
        lax.all_gather(stacked[8][layer_index], "shard", axis=0, tiled=True),
    )


def attention_scores(queries, keys_rot, mask):
    scores = jnp.einsum(
        "qkgd,tkd->kgqt", queries, keys_rot, preferred_element_type=jnp.float32
    ) * HEAD ** (-0.5)
    return jnp.where(mask, scores, masked_score)


def layer_forward(stream, weights, mask, cosine, sine):
    (
        attention_gain,
        query_weight,
        key_weight,
        value_weight,
        output_weight,
        feedforward_gain,
        gate_weight,
        up_weight,
        down_weight,
    ) = weights
    row_count = stream.shape[0]
    group_size = HEADS // KV_HEADS
    scale_one = rms_scale(stream)
    normed_one = (stream * scale_one * attention_gain.astype(jnp.float32)).astype(jnp.bfloat16)
    queries = left_product(normed_one, query_weight).reshape(row_count, HEADS, HEAD)
    queries = (
        rotate(queries, cosine, sine)
        .astype(jnp.bfloat16)
        .reshape(row_count, KV_HEADS, group_size, HEAD)
    )
    keys_rot = left_product(normed_one, key_weight).reshape(row_count, KV_HEADS, HEAD)
    keys_rot = rotate(keys_rot, cosine, sine).astype(jnp.bfloat16)
    values = (
        left_product(normed_one, value_weight)
        .astype(jnp.bfloat16)
        .reshape(row_count, KV_HEADS, HEAD)
    )
    scores = attention_scores(queries, keys_rot, mask)
    row_max = jnp.max(scores, axis=-1, keepdims=True)
    shifted = jnp.exp(scores - row_max)
    row_total = jnp.sum(shifted, axis=-1, keepdims=True)
    attention = shifted / row_total
    log_total = row_max + jnp.log(row_total)
    mixed = jnp.einsum(
        "kgqt,tkd->qkgd", attention.astype(jnp.bfloat16), values, preferred_element_type=jnp.float32
    )
    mixed = mixed.reshape(row_count, HEADS * HEAD).astype(jnp.bfloat16)
    middle = stream + left_product(mixed, output_weight)
    scale_two = rms_scale(middle)
    normed_two = (middle * scale_two * feedforward_gain.astype(jnp.float32)).astype(jnp.bfloat16)
    gate_lin = left_product(normed_two, gate_weight)
    up_lin = left_product(normed_two, up_weight)
    hidden = (gate_lin * jax.nn.sigmoid(gate_lin) * up_lin).astype(jnp.bfloat16)
    result_stream = middle + left_product(hidden, down_weight)
    kept = (
        stream,
        scale_one,
        normed_one,
        queries,
        keys_rot,
        values,
        log_total,
        mixed,
        middle,
        scale_two,
        normed_two,
        gate_lin,
        up_lin,
        hidden,
    )
    return (result_stream, kept)


def layer_backward(grad_out, weights, kept, mask, cosine, sine):
    (
        attention_gain,
        query_weight,
        key_weight,
        value_weight,
        output_weight,
        feedforward_gain,
        gate_weight,
        up_weight,
        down_weight,
    ) = weights
    (
        stream,
        scale_one,
        normed_one,
        queries,
        keys_rot,
        values,
        log_total,
        mixed,
        middle,
        scale_two,
        normed_two,
        gate_lin,
        up_lin,
        hidden,
    ) = kept
    row_count = stream.shape[0]
    group_size = HEADS // KV_HEADS
    branch_grad = grad_out.astype(jnp.bfloat16)
    hidden_grad = right_transposed(branch_grad, down_weight)
    down_grad = row_sum_product(hidden, branch_grad)
    sigma = jax.nn.sigmoid(gate_lin)
    gate_grad = (hidden_grad * up_lin * sigma * (1.0 + gate_lin * (1.0 - sigma))).astype(
        jnp.bfloat16
    )
    up_grad = (hidden_grad * gate_lin * sigma).astype(jnp.bfloat16)
    normed_grad = right_transposed(gate_grad, gate_weight) + right_transposed(up_grad, up_weight)
    gate_weight_grad = row_sum_product(normed_two, gate_grad)
    up_weight_grad = row_sum_product(normed_two, up_grad)
    forward_gain_grad, middle_part = norm_backward(normed_grad, middle, scale_two, feedforward_gain)
    middle_grad = grad_out + middle_part
    mlp_shares = (
        lax.psum_scatter(
            forward_gain_grad.astype(jnp.bfloat16), "shard", scatter_dimension=0, tiled=True
        ).astype(jnp.float32),
        lax.psum_scatter(
            gate_weight_grad.astype(jnp.bfloat16), "shard", scatter_dimension=0, tiled=True
        ).astype(jnp.float32),
        lax.psum_scatter(
            up_weight_grad.astype(jnp.bfloat16), "shard", scatter_dimension=0, tiled=True
        ).astype(jnp.float32),
        lax.psum_scatter(
            down_grad.astype(jnp.bfloat16), "shard", scatter_dimension=0, tiled=True
        ).astype(jnp.float32),
    )
    branch_grad = middle_grad.astype(jnp.bfloat16)
    mixed_grad = right_transposed(branch_grad, output_weight).astype(jnp.bfloat16)
    output_weight_grad = row_sum_product(mixed, branch_grad)
    mixed_grad = mixed_grad.reshape(row_count, KV_HEADS, group_size, HEAD)
    scores = attention_scores(queries, keys_rot, mask)
    attention = jnp.exp(scores - log_total)
    attention_grad = jnp.einsum(
        "qkgd,tkd->kgqt", mixed_grad, values, preferred_element_type=jnp.float32
    )
    value_grad = jnp.einsum(
        "kgqt,qkgd->tkd",
        attention.astype(jnp.bfloat16),
        mixed_grad,
        preferred_element_type=jnp.float32,
    )
    value_grad = value_grad.astype(jnp.bfloat16).reshape(row_count, KV_HEADS * HEAD)
    row_dot = jnp.sum(attention * attention_grad, axis=-1, keepdims=True)
    score_grad = (attention * (attention_grad - row_dot)).astype(jnp.bfloat16)
    query_grad = jnp.einsum(
        "kgqt,tkd->qkgd", score_grad, keys_rot, preferred_element_type=jnp.float32
    ) * HEAD ** (-0.5)
    key_grad = jnp.einsum(
        "kgqt,qkgd->tkd", score_grad, queries, preferred_element_type=jnp.float32
    ) * HEAD ** (-0.5)
    query_grad = (
        unrotate(query_grad.reshape(row_count, HEADS, HEAD), cosine, sine)
        .astype(jnp.bfloat16)
        .reshape(row_count, HEADS * HEAD)
    )
    key_grad = (
        unrotate(key_grad, cosine, sine).astype(jnp.bfloat16).reshape(row_count, KV_HEADS * HEAD)
    )
    normed_grad = (
        right_transposed(query_grad, query_weight)
        + right_transposed(key_grad, key_weight)
        + right_transposed(value_grad, value_weight)
    )
    query_weight_grad = row_sum_product(normed_one, query_grad)
    key_weight_grad = row_sum_product(normed_one, key_grad)
    value_weight_grad = row_sum_product(normed_one, value_grad)
    attend_gain_grad, stream_part = norm_backward(normed_grad, stream, scale_one, attention_gain)
    attention_shares = (
        lax.psum_scatter(
            attend_gain_grad.astype(jnp.bfloat16), "shard", scatter_dimension=0, tiled=True
        ).astype(jnp.float32),
        lax.psum_scatter(
            query_weight_grad.astype(jnp.bfloat16), "shard", scatter_dimension=0, tiled=True
        ).astype(jnp.float32),
        lax.psum_scatter(
            key_weight_grad.astype(jnp.bfloat16), "shard", scatter_dimension=0, tiled=True
        ).astype(jnp.float32),
        lax.psum_scatter(
            value_weight_grad.astype(jnp.bfloat16), "shard", scatter_dimension=0, tiled=True
        ).astype(jnp.float32),
        lax.psum_scatter(
            output_weight_grad.astype(jnp.bfloat16), "shard", scatter_dimension=0, tiled=True
        ).astype(jnp.float32),
    )
    return (middle_grad + stream_part, attention_shares + mlp_shares)


def shards(
    tokens,
    cotangent,
    lengths,
    deal_order,
    attention_gain,
    query_weight,
    key_weight,
    value_weight,
    output_weight,
    feedforward_gain,
    gate_weight,
    up_weight,
    down_weight,
):
    stacked = (
        attention_gain,
        query_weight,
        key_weight,
        value_weight,
        output_weight,
        feedforward_gain,
        gate_weight,
        up_weight,
        down_weight,
    )
    shard_count = lax.axis_size("shard")
    device = lax.axis_index(("rep", "shard"))
    wanted = deal_order[device]
    length = lengths[wanted]
    sequence = pick_sequence(
        wanted // shard_count,
        jnp.zeros_like(tokens),
        lax.all_gather(tokens, "rep", axis=0, tiled=True),
    )
    row_count = tokens.shape[1]
    position = jnp.arange(row_count)
    valid = (position < length)[:, None]
    mask = (position[None, :] <= position[:, None]) & (position[None, :] < length)
    cosine, sine = rope_tables(row_count)
    stream = sequence[0].astype(jnp.float32)
    kept_layers = []
    weights = None
    for layer_index in range(LAYERS):
        weights = gather_forward(stacked, layer_index)
        stream, kept = layer_forward(stream, weights, mask, cosine, sine)
        kept_layers.append(kept)
    layer_output = jnp.where(valid, stream, 0.0).astype(jnp.bfloat16)[None]
    grad_stream = jnp.where(valid, cotangent[0].astype(jnp.float32), 0.0)
    layer_shares = [None] * LAYERS
    for layer_index in reversed(range(LAYERS)):
        weights_back = gather_backward(stacked, layer_index)
        grad_stream, shares = layer_backward(
            grad_stream, weights_back, kept_layers[layer_index], mask, cosine, sine
        )
        layer_shares[layer_index] = shares
    grads = tuple(
        (jnp.stack([layer_shares[index][member] for index in range(LAYERS)]) for member in range(9))
    )
    grads = (
        lax.psum(grads[0].astype(jnp.bfloat16), "rep").astype(jnp.float32),
        lax.psum(grads[1].astype(jnp.bfloat16), "rep").astype(jnp.float32),
        lax.psum(grads[2].astype(jnp.bfloat16), "rep").astype(jnp.float32),
        lax.psum(grads[3].astype(jnp.bfloat16), "rep").astype(jnp.float32),
        lax.psum(grads[4].astype(jnp.bfloat16), "rep").astype(jnp.float32),
        lax.psum(grads[5].astype(jnp.bfloat16), "rep").astype(jnp.float32),
        lax.psum(grads[6].astype(jnp.bfloat16), "rep").astype(jnp.float32),
        lax.psum(grads[7].astype(jnp.bfloat16), "rep").astype(jnp.float32),
        lax.psum(grads[8].astype(jnp.bfloat16), "rep").astype(jnp.float32),
    )
    inverse = jnp.sum(jnp.where(deal_order == device, jnp.arange(deal_order.shape[0]), 0))
    input_grad = pick_sequence(
        inverse // shard_count,
        jnp.zeros_like(tokens),
        lax.all_gather(grad_stream.astype(jnp.bfloat16)[None], "rep", axis=0, tiled=True),
    )
    return (layer_output, input_grad) + tuple(grads)


def solution(mesh):
    placed = (
        P(("rep", "shard"), None, None),
        P(("rep", "shard"), None, None),
        P(),
        P(),
        P(None, "shard"),
        P(None, "shard", None),
        P(None, "shard", None),
        P(None, "shard", None),
        P(None, "shard", None),
        P(None, "shard"),
        P(None, "shard", None),
        P(None, "shard", None),
        P(None, "shard", None),
    )
    return jax.shard_map(
        shards,
        mesh=mesh,
        in_specs=placed,
        out_specs=(
            P(("rep", "shard"), None, None),
            P(("rep", "shard"), None, None),
            P(None, "shard"),
            P(None, "shard", None),
            P(None, "shard", None),
            P(None, "shard", None),
            P(None, "shard", None),
            P(None, "shard"),
            P(None, "shard", None),
            P(None, "shard", None),
            P(None, "shard", None),
        ),
        check_vma=False,
    )
```

profile of v0, /device:TPU:0, one launch (start us, length us, event | category | flops | bytes accessed | tf_op | source)
XLA Modules:
  0.0 4235.6 jit_solution(707342799464342113)
XLA Ops:
  45.1 15.0 all-gather.14
  60.2 11.9 all-gather.9
  72.1 11.9 all-gather.5
  84.0 11.9 all-gather
  104.3 43.7 %all-gather.38.cloned.1.call-done = bf16[1,1536,768]{2,1,0:T(8,128)(2,1)} async-done(((bf16[1,384,768]{2,1,0:T(8,128)(2,1)}), bf16[1,1536,768]{2,1,0:T(8,128)(2,1)}) %all-gather.38.cloned.1.call-update) | async-done | bytes 2359312 | tf_op jit(solution)/shard_map/all_gather | solution.py:75
  153.4 84.8 %all-gather.42.cloned.1.call-done = bf16[1,1536,1536]{2,1,0:T(8,128)(2,1)} async-done(((bf16[1,384,1536]{2,1,0:T(8,128)(2,1)}), bf16[1,1536,1536]{2,1,0:T(8,128)(2,1)}) %all-gather.42.cloned.1.call-update) | async-done | bytes 4718608 | tf_op jit(solution)/shard_map/all_gather | solution.py:73
  251.2 76.2 %all-gather.44.cloned.1.call-done = bf16[1,1536,1536]{2,1,0:T(8,128)(2,1)} async-done(((bf16[1,384,1536]{2,1,0:T(8,128)(2,1)}), bf16[1,1536,1536]{2,1,0:T(8,128)(2,1)}) %all-gather.44.cloned.1.call-update) | async-done | bytes 4718608 | tf_op jit(solution)/shard_map/all_gather | solution.py:76
  332.1 214.0 %all-gather.46.cloned.1.call-done = bf16[1,1536,4096]{2,1,0:T(8,128)(2,1)} async-done(((bf16[1,384,4096]{2,1,0:T(8,128)(2,1)}), bf16[1,1536,4096]{2,1,0:T(8,128)(2,1)}) %all-gather.46.cloned.1.call-update) | async-done | bytes 12582928 | tf_op jit(solution)/shard_map/all_gather | solution.py:78
  553.8 210.8 %all-gather.48.cloned.1.call-done = bf16[1,1536,4096]{2,1,0:T(8,128)(2,1)} async-done(((bf16[1,384,4096]{2,1,0:T(8,128)(2,1)}), bf16[1,1536,4096]{2,1,0:T(8,128)(2,1)}) %all-gather.48.cloned.1.call-update) | async-done | bytes 12582928 | tf_op jit(solution)/shard_map/all_gather | solution.py:79
  773.6 209.0 %all-gather.50.cloned.1.call-done = bf16[1,4096,1536]{2,1,0:T(8,128)(2,1)} async-done(((bf16[1,1024,1536]{2,1,0:T(8,128)(2,1)}), bf16[1,4096,1536]{2,1,0:T(8,128)(2,1)}) %all-gather.50.cloned.1.call-update) | async-done | bytes 12582928 | tf_op jit(solution)/shard_map/all_gather | solution.py:80
  990.2 42.2 all-gather.52.cloned.1.call-done
  1035.3 47.2 %all-gather.54.cloned.1.call-done = bf16[1,1536,768]{2,1,0:T(8,128)(2,1)} async-done(((bf16[1,384,768]{2,1,0:T(8,128)(2,1)}), bf16[1,1536,768]{2,1,0:T(8,128)(2,1)}) %all-gather.54.cloned.1.call-update) | async-done | bytes 2359312 | tf_op jit(solution)/shard_map/all_gather | solution.py:74
  1086.1 86.2 %all-gather.56.cloned.1.call-done = bf16[1,1536,1536]{2,1,0:T(8,128)(2,1)} async-done(((bf16[1,384,1536]{2,1,0:T(8,128)(2,1)}), bf16[1,1536,1536]{2,1,0:T(8,128)(2,1)}) %all-gather.56.cloned.1.call-update) | async-done | bytes 4718608 | tf_op jit(solution)/shard_map/all_gather | solution.py:73
  1179.4 82.2 %all-gather.58.cloned.1.call-done = bf16[1,1536,1536]{2,1,0:T(8,128)(2,1)} async-done(((bf16[1,384,1536]{2,1,0:T(8,128)(2,1)}), bf16[1,1536,1536]{2,1,0:T(8,128)(2,1)}) %all-gather.58.cloned.1.call-update) | async-done | bytes 4718608 | tf_op jit(solution)/shard_map/all_gather | solution.py:76
  1266.2 214.2 %all-gather.62.cloned.1.call-done = bf16[1,1536,4096]{2,1,0:T(8,128)(2,1)} async-done(((bf16[1,384,4096]{2,1,0:T(8,128)(2,1)}), bf16[1,1536,4096]{2,1,0:T(8,128)(2,1)}) %all-gather.62.cloned.1.call-update) | async-done | bytes 12582928 | tf_op jit(solution)/shard_map/all_gather | solution.py:79
  1488.2 210.0 %all-gather.64.cloned.1.call-done = bf16[1,4096,1536]{2,1,0:T(8,128)(2,1)} async-done(((bf16[1,1024,1536]{2,1,0:T(8,128)(2,1)}), bf16[1,4096,1536]{2,1,0:T(8,128)(2,1)}) %all-gather.64.cloned.1.call-update) | async-done | bytes 12582928 | tf_op jit(solution)/shard_map/all_gather | solution.py:80
  1708.4 208.2 %all-gather.60.cloned.1.call-done = bf16[1,1536,4096]{2,1,0:T(8,128)(2,1)} async-done(((bf16[1,384,4096]{2,1,0:T(8,128)(2,1)}), bf16[1,1536,4096]{2,1,0:T(8,128)(2,1)}) %all-gather.60.cloned.1.call-update) | async-done | bytes 12582928 | tf_op jit(solution)/shard_map/all_gather | solution.py:78
  2097.9 47.4 %reduce-scatter.19.cloned.1.call-done = bf16[384,768]{1,0:T(8,128)(2,1)} async-done(((bf16[1536,768]{1,0:T(8,128)(2,1)}), bf16[384,768]{1,0:T(8,128)(2,1)}) %reduce-scatter.19.cloned.1.call-update) | async-done | bytes 589840 | tf_op jit(solution)/shard_map/reduce_scatter | solution.py:275
  2145.3 50.0 %reduce-scatter.21.cloned.1.call-done = bf16[384,768]{1,0:T(8,128)(2,1)} async-done(((bf16[1536,768]{1,0:T(8,128)(2,1)}), bf16[384,768]{1,0:T(8,128)(2,1)}) %reduce-scatter.21.cloned.1.call-update) | async-done | bytes 589840 | tf_op jit(solution)/shard_map/reduce_scatter | solution.py:275
  2197.7 84.5 %reduce-scatter.27.cloned.1.call-done = bf16[384,1536]{1,0:T(8,128)(2,1)} async-done(((bf16[1536,1536]{1,0:T(8,128)(2,1)}), bf16[384,1536]{1,0:T(8,128)(2,1)}) %reduce-scatter.27.cloned.1.call-update) | async-done | bytes 1179664 | tf_op jit(solution)/shard_map/reduce_scatter | solution.py:281
  2282.2 88.2 %reduce-scatter.29.cloned.1.call-done = bf16[384,1536]{1,0:T(8,128)(2,1)} async-done(((bf16[1536,1536]{1,0:T(8,128)(2,1)}), bf16[384,1536]{1,0:T(8,128)(2,1)}) %reduce-scatter.29.cloned.1.call-update) | async-done | bytes 1179664 | tf_op jit(solution)/shard_map/reduce_scatter | solution.py:281
  2373.6 85.5 %reduce-scatter.15.cloned.1.call-done = bf16[384,1536]{1,0:T(8,128)(2,1)} async-done(((bf16[1536,1536]{1,0:T(8,128)(2,1)}), bf16[384,1536]{1,0:T(8,128)(2,1)}) %reduce-scatter.15.cloned.1.call-update) | async-done | bytes 1179664 | tf_op jit(solution)/shard_map/reduce_scatter | solution.py:272
  2459.0 88.7 %reduce-scatter.17.cloned.1.call-done = bf16[384,1536]{1,0:T(8,128)(2,1)} async-done(((bf16[1536,1536]{1,0:T(8,128)(2,1)}), bf16[384,1536]{1,0:T(8,128)(2,1)}) %reduce-scatter.17.cloned.1.call-update) | async-done | bytes 1179664 | tf_op jit(solution)/shard_map/reduce_scatter | solution.py:272
  2551.0 211.4 %reduce-scatter.39.cloned.1.call-done = bf16[1024,1536]{1,0:T(8,128)(2,1)} async-done(((bf16[4096,1536]{1,0:T(8,128)(2,1)}), bf16[1024,1536]{1,0:T(8,128)(2,1)}) %reduce-scatter.39.cloned.1.call-update) | async-done | bytes 3145744 | tf_op jit(solution)/shard_map/reduce_scatter | solution.py:223
  2762.4 215.3 %reduce-scatter.41.cloned.1.call-done = bf16[1024,1536]{1,0:T(8,128)(2,1)} async-done(((bf16[4096,1536]{1,0:T(8,128)(2,1)}), bf16[1024,1536]{1,0:T(8,128)(2,1)}) %reduce-scatter.41.cloned.1.call-update) | async-done | bytes 3145744 | tf_op jit(solution)/shard_map/reduce_scatter | solution.py:223
  2983.7 209.7 %reduce-scatter.31.cloned.1.call-done = bf16[384,4096]{1,0:T(8,128)(2,1)} async-done(((bf16[1536,4096]{1,0:T(8,128)(2,1)}), bf16[384,4096]{1,0:T(8,128)(2,1)}) %reduce-scatter.31.cloned.1.call-update) | async-done | bytes 3145744 | tf_op jit(solution)/shard_map/reduce_scatter | solution.py:217
  3193.4 215.7 %reduce-scatter.33.cloned.1.call-done = bf16[384,4096]{1,0:T(8,128)(2,1)} async-done(((bf16[1536,4096]{1,0:T(8,128)(2,1)}), bf16[384,4096]{1,0:T(8,128)(2,1)}) %reduce-scatter.33.cloned.1.call-update) | async-done | bytes 3145744 | tf_op jit(solution)/shard_map/reduce_scatter | solution.py:217
  3415.3 209.2 %reduce-scatter.35.cloned.1.call-done = bf16[384,4096]{1,0:T(8,128)(2,1)} async-done(((bf16[1536,4096]{1,0:T(8,128)(2,1)}), bf16[384,4096]{1,0:T(8,128)(2,1)}) %reduce-scatter.35.cloned.1.call-update) | async-done | bytes 3145744 | tf_op jit(solution)/shard_map/reduce_scatter | solution.py:220
  3624.5 215.9 %reduce-scatter.37.cloned.1.call-done = bf16[384,4096]{1,0:T(8,128)(2,1)} async-done(((bf16[1536,4096]{1,0:T(8,128)(2,1)}), bf16[384,4096]{1,0:T(8,128)(2,1)}) %reduce-scatter.37.cloned.1.call-update) | async-done | bytes 3145744 | tf_op jit(solution)/shard_map/reduce_scatter | solution.py:220
  3851.6 18.5 all-reduce.6
  3870.5 12.0 all-reduce.4
  3892.9 305.1 %all-reduce.9.cloned.1.call-done = (bf16[2,384,1536]{2,1,0:T(8,128)(2,1)}, bf16[2,384,768]{2,1,0:T(8,128)(2,1)}, bf16[2,384,768]{2,1,0:T(8,128)(2,1)}, bf16[2,38...) async-done(((bf16[2,384,1536]{2,1,0:T(8,128)(2,1)}, bf16[2,384,768]{2,1,0:T(8,128)(2,1)}, ...) | async-done | bytes 25952272 | tf_op jit(solution)/shard_map/psum | solution.py:349
  (420 shorter events, 376.0 us)
Async XLA Ops:
  7.2 91.2 %all-gather.40.cloned.1.call-start = ((), (), s32[]{:S(2)}) async-start(), calls=%async_computation.30 | async-start | bytes 2949120 | tf_op jit(solution)/shard_map/all_gather | solution.py:74
  9.7 92.9 %all-gather.36.cloned.1.call-start = ((), (), s32[]{:S(2)}) async-start(), calls=%async_computation.14 | async-start | bytes 3538944 | tf_op jit(solution)/shard_map/all_gather | solution.py:321
  10.5 137.5 %all-gather.38.cloned.1.call-start = ((), (), s32[]{:S(2)}) async-start(), calls=%async_computation.29 | async-start | bytes 2949120 | tf_op jit(solution)/shard_map/all_gather | solution.py:75
  11.7 226.5 %all-gather.42.cloned.1.call-start = ((), (), s32[]{:S(2)}) async-start(), calls=%async_computation.31 | async-start | bytes 5898240 | tf_op jit(solution)/shard_map/all_gather | solution.py:73
  13.3 314.1 %all-gather.44.cloned.1.call-start = ((), (), s32[]{:S(2)}) async-start(), calls=%async_computation.32 | async-start | bytes 5898240 | tf_op jit(solution)/shard_map/all_gather | solution.py:76
  16.6 529.5 %all-gather.46.cloned.1.call-start = ((), (), s32[]{:S(2)}) async-start(), calls=%async_computation.33 | async-start | bytes 15728640 | tf_op jit(solution)/shard_map/all_gather | solution.py:78
  23.0 741.6 %all-gather.48.cloned.1.call-start = ((), (), s32[]{:S(2)}) async-start(), calls=%async_computation.34 | async-start | bytes 15728640 | tf_op jit(solution)/shard_map/all_gather | solution.py:79
  29.4 953.1 %all-gather.50.cloned.1.call-start = ((), (), s32[]{:S(2)}) async-start(), calls=%async_computation.35 | async-start | bytes 15728640 | tf_op jit(solution)/shard_map/all_gather | solution.py:80
  35.4 997.0 %all-gather.52.cloned.1.call-start = ((), (), s32[]{:S(2)}) async-start(), calls=%async_computation.36 | async-start | bytes 2949120 | tf_op jit(solution)/shard_map/all_gather | solution.py:75
  36.1 1046.4 %all-gather.54.cloned.1.call-start = ((), (), s32[]{:S(2)}) async-start(), calls=%async_computation.37 | async-start | bytes 2949120 | tf_op jit(solution)/shard_map/all_gather | solution.py:74
  36.7 1135.6 %all-gather.56.cloned.1.call-start = ((), (), s32[]{:S(2)}) async-start(), calls=%async_computation.38 | async-start | bytes 5898240 | tf_op jit(solution)/shard_map/all_gather | solution.py:73
  37.5 1224.1 %all-gather.58.cloned.1.call-start = ((), (), s32[]{:S(2)}) async-start(), calls=%async_computation.39 | async-start | bytes 5898240 | tf_op jit(solution)/shard_map/all_gather | solution.py:76
  38.0 1442.3 %all-gather.62.cloned.1.call-start = ((), (), s32[]{:S(2)}) async-start(), calls=%async_computation.41 | async-start | bytes 15728640 | tf_op jit(solution)/shard_map/all_gather | solution.py:79
  38.8 1659.4 %all-gather.64.cloned.1.call-start = ((), (), s32[]{:S(2)}) async-start(), calls=%async_computation.42 | async-start | bytes 15728640 | tf_op jit(solution)/shard_map/all_gather | solution.py:80
  39.4 1877.2 %all-gather.60.cloned.1.call-start = ((), (), s32[]{:S(2)}) async-start(), calls=%async_computation.40 | async-start | bytes 15728640 | tf_op jit(solution)/shard_map/all_gather | solution.py:78
  40.0 2051.7 %reduce-scatter.23.cloned.1.call-start = ((), (), s32[]{:S(2)}) async-start(), calls=%async_computation.19 | async-start | bytes 2949120 | tf_op jit(solution)/shard_map/reduce_scatter | solution.py:278
  98.2 1853.7 %copy-start.33 = (f32[128,96]{0,1:T(8,128)}, f32[128,96]{0,1:T(8,128)S(1)}, u32[]{:S(2)}) copy-start(f32[128,96]{0,1:T(8,128)S(1)} %get-tuple-element.71) | copy-start | bytes 147460
  2000.2 95.3 %reduce-scatter.25.cloned.1.call-start = ((), (), s32[]{:S(2)}) async-start(), calls=%async_computation.20 | async-start | bytes 2949120 | tf_op jit(solution)/shard_map/reduce_scatter | solution.py:278
  2002.5 142.8 %reduce-scatter.19.cloned.1.call-start = ((), (), s32[]{:S(2)}) async-start(), calls=%async_computation.17 | async-start | bytes 2949120 | tf_op jit(solution)/shard_map/reduce_scatter | solution.py:275
  2007.9 187.4 %reduce-scatter.21.cloned.1.call-start = ((), (), s32[]{:S(2)}) async-start(), calls=%async_computation.18 | async-start | bytes 2949120 | tf_op jit(solution)/shard_map/reduce_scatter | solution.py:275
  2010.2 272.0 %reduce-scatter.27.cloned.1.call-start = ((), (), s32[]{:S(2)}) async-start(), calls=%async_computation.21 | async-start | bytes 5898240 | tf_op jit(solution)/shard_map/reduce_scatter | solution.py:281
  2013.8 356.5 %reduce-scatter.29.cloned.1.call-start = ((), (), s32[]{:S(2)}) async-start(), calls=%async_computation.22 | async-start | bytes 5898240 | tf_op jit(solution)/shard_map/reduce_scatter | solution.py:281
  2018.6 440.5 %reduce-scatter.15.cloned.1.call-start = ((), (), s32[]{:S(2)}) async-start(), calls=%async_computation.15 | async-start | bytes 5898240 | tf_op jit(solution)/shard_map/reduce_scatter | solution.py:272
  2025.8 522.0 %reduce-scatter.17.cloned.1.call-start = ((), (), s32[]{:S(2)}) async-start(), calls=%async_computation.16 | async-start | bytes 5898240 | tf_op jit(solution)/shard_map/reduce_scatter | solution.py:272
  2030.4 732.0 %reduce-scatter.39.cloned.1.call-start = ((), (), s32[]{:S(2)}) async-start(), calls=%async_computation.27 | async-start | bytes 15728640 | tf_op jit(solution)/shard_map/reduce_scatter | solution.py:223
  2038.7 939.0 %reduce-scatter.41.cloned.1.call-start = ((), (), s32[]{:S(2)}) async-start(), calls=%async_computation.28 | async-start | bytes 15728640 | tf_op jit(solution)/shard_map/reduce_scatter | solution.py:223
  2046.6 1146.8 %reduce-scatter.31.cloned.1.call-start = ((), (), s32[]{:S(2)}) async-start(), calls=%async_computation.23 | async-start | bytes 15728640 | tf_op jit(solution)/shard_map/reduce_scatter | solution.py:217
  2055.4 1353.7 %reduce-scatter.33.cloned.1.call-start = ((), (), s32[]{:S(2)}) async-start(), calls=%async_computation.24 | async-start | bytes 15728640 | tf_op jit(solution)/shard_map/reduce_scatter | solution.py:217
  2064.2 1560.2 %reduce-scatter.35.cloned.1.call-start = ((), (), s32[]{:S(2)}) async-start(), calls=%async_computation.25 | async-start | bytes 15728640 | tf_op jit(solution)/shard_map/reduce_scatter | solution.py:220
  2072.3 1768.0 %reduce-scatter.37.cloned.1.call-start = ((), (), s32[]{:S(2)}) async-start(), calls=%async_computation.26 | async-start | bytes 15728640 | tf_op jit(solution)/shard_map/reduce_scatter | solution.py:220
  2080.2 1810.9 %all-gather.66.cloned.1.call-start = ((), (), s32[]{:S(2)}) async-start(), calls=%async_computation.43 | async-start | bytes 3538944 | tf_op jit(solution)/shard_map/all_gather | solution.py:362
  2091.6 2106.3 %all-reduce.9.cloned.1.call-start = ((), (), s32[]{:S(2)}) async-start(), calls=%async_computation.44 | async-start | bytes 51904512 | tf_op jit(solution)/shard_map/psum | solution.py:349
  (97 other events, 4376.3 us)
Sparse Core Ops, SparseCore 0:
  10.1 52.8 all-gather.39
  64.9 30.9 all-gather.35
  98.0 49.9 all-gather.37
  150.0 88.1 all-gather.41
  239.6 87.7 all-gather.43
  329.4 216.5 all-gather.45
  548.2 216.3 all-gather.47
  766.2 216.3 all-gather.49
  984.2 48.1 all-gather.51
  1033.8 48.7 all-gather.53
  1084.1 88.1 all-gather.55
  1173.7 87.7 all-gather.57
  1263.7 216.5 all-gather.61
  1481.8 216.3 all-gather.63
  1700.1 216.3 all-gather.59
  2000.3 45.8 reduce-scatter.22
  2048.4 47.0 reduce-scatter.24
  2098.2 47.0 reduce-scatter.18
  2148.2 47.0 reduce-scatter.20
  2197.5 84.6 reduce-scatter.26
  2284.5 85.7 reduce-scatter.28
  2373.2 85.7 reduce-scatter.14
  2461.9 85.7 reduce-scatter.16
  2550.0 212.3 reduce-scatter.38
  2764.8 212.8 reduce-scatter.40
  2980.5 212.8 reduce-scatter.30
  3196.2 212.8 reduce-scatter.32
  3411.5 212.8 reduce-scatter.34
  3627.4 212.8 reduce-scatter.36
  3842.6 33.1 all-gather.65
  3882.2 315.6 all-reduce.8
where the time goes:
time: 4240 us
  waiting for transfers between devices  3760 us (89%)
  matrix products  228 us (5%)
  blocking collectives  81.3 us (2%)
  other arithmetic  79.8 us (2%)
  local copies, waits for them, and re-layouts  57.7 us (1%)
    reduce_scatter x2, waiting for transfers between devices, layer_backward(): lax.psum_scatter(down_grad.astype(jnp.bfloat16), 'shard', scatter_dimensi...  427 us
    reduce_scatter x2, waiting for transfers between devices, layer_backward(): lax.psum_scatter(gate_weight_grad.astype(jnp.bfloat16), 'shard', scatter_...  425 us
    reduce_scatter x2, waiting for transfers between devices, layer_backward(): lax.psum_scatter(up_weight_grad.astype(jnp.bfloat16), 'shard', scatter_di...  425 us
    all_gather x2, waiting for transfers between devices, gather_forward(): lax.all_gather(stacked[7][layer_index], 'shard', axis=0, tiled=True)  425 us
    all_gather x2, waiting for transfers between devices, gather_forward(): lax.all_gather(stacked[6][layer_index], 'shard', axis=0, tiled=True)  422 us
    all_gather x2, waiting for transfers between devices, gather_forward(): lax.all_gather(stacked[8][layer_index], 'shard', axis=0, tiled=True)  419 us
    psum x1, waiting for transfers between devices, shards(): lax.psum(grads[1].astype(jnp.bfloat16), 'rep').astype(jnp.float32)  305 us
    reduce_scatter x2, waiting for transfers between devices, layer_backward(): lax.psum_scatter(query_weight_grad.astype(jnp.bfloat16), 'shard', scatter...  174 us
  transfers between devices with their start and end apart: 31, of which 27 were waited for; matrix products, arithmetic and copies ran while one was open for 6% of the time, Pallas kernels for 0%

commit v1 on v0

--- a/solution.py
+++ b/solution.py
@@ -1,6 +1,9 @@
+import functools
 import jax
 import jax.numpy as jnp
 from jax import lax
+from jax.experimental import pallas as pl
+from jax.experimental.pallas import tpu as pltpu
 from jax.sharding import PartitionSpec as P
 
 HEADS = 16
@@ -285,7 +288,7 @@
     return (middle_grad + stream_part, attention_shares + mlp_shares)
 
 
-def shards(
+def whole_weight_shards(
     tokens,
     cotangent,
     lengths,
@@ -364,6 +367,528 @@
     return (layer_output, input_grad) + tuple(grads)
 
 
+PIECES = 4
+MESH = pl.DeviceIdType.MESH
+
+
+def plane_neighbours():
+    place = lax.axis_index("rep")
+    core, chip = place % 2, place // 2
+    mate = place + 1 - 2 * core
+    across = place + 2 - 4 * (chip % 2)
+    along = place + 4 - 8 * (chip // 2)
+    return (place, mate, across, along)
+
+
+def remote(source, target, sems, kind, piece, place):
+    send_sem, recv_sem = sems
+    copy = pltpu.make_async_remote_copy(
+        src_ref=source,
+        dst_ref=target,
+        send_sem=send_sem.at[kind, piece],
+        recv_sem=recv_sem.at[kind, piece],
+        device_id={"rep": place},
+        device_id_type=MESH,
+    )
+    copy.start()
+    return copy
+
+
+def greet(places):
+    barrier = pltpu.get_barrier_semaphore()
+    for place in places:
+        pl.semaphore_signal(barrier, inc=1, device_id=place, device_id_type=MESH)
+    pl.semaphore_wait(barrier, len(places))
+
+
+def piece_rows(piece, row_count):
+    span = row_count // PIECES
+    return (pl.ds(piece * span, span), pl.ds(piece * span, span // 2), pl.ds(piece * span + span // 2, span // 2))
+
+
+def gather_send(full, sems, first_kind, piece, row_count):
+    place, mate, across, along = plane_neighbours()
+    rows, _, _ = piece_rows(piece, row_count)
+    own = full.at[place, rows]
+    return [
+        remote(own, own, sems, first_kind, piece, mate),
+        remote(own, own, sems, first_kind + 1, piece, across),
+        remote(own, own, sems, first_kind + 2, piece, along),
+    ]
+
+
+def gather_finish(full, sems, first_kind, row_count, sent):
+    place, mate, across, along = plane_neighbours()
+    far = across + along - place
+    passed = []
+    for piece in range(PIECES):
+        rows, upper, lower = piece_rows(piece, row_count)
+        sent[piece][1].wait_recv()
+        there = full.at[across, upper]
+        whole = full.at[across, rows]
+        to_along = remote(there, there, sems, first_kind + 3, piece, along)
+        mate_one = remote(whole, whole, sems, first_kind + 5, piece, mate)
+        sent[piece][2].wait_recv()
+        there = full.at[along, lower]
+        whole = full.at[along, rows]
+        to_across = remote(there, there, sems, first_kind + 4, piece, across)
+        mate_two = remote(whole, whole, sems, first_kind + 6, piece, mate)
+        passed.append([to_along, to_across, mate_one, mate_two])
+    for piece in range(PIECES):
+        rows, _, _ = piece_rows(piece, row_count)
+        passed[piece][0].wait_recv()
+        passed[piece][1].wait_recv()
+        whole = full.at[far, rows]
+        passed[piece].append(remote(whole, whole, sems, first_kind + 7, piece, mate))
+    for piece in range(PIECES):
+        sent[piece][0].wait_recv()
+        for copy in passed[piece][2:]:
+            copy.wait_recv()
+        for copy in sent[piece] + passed[piece]:
+            copy.wait_send()
+
+
+def scatter_stage(left, right, transposed, part, from_mate, send_far, send_across, send_along,
+                  far_across, far_along, got_across, got_along, sems, finish):
+    place, mate, across, along = plane_neighbours()
+    core, chip = place % 2, place // 2
+    far_chip, across_chip, along_chip = (across + along - place) // 2, across // 2, along // 2
+    row_count, width = part.shape[2], part.shape[3]
+    span = row_count // PIECES
+    depth = left.shape[-1]
+    wide = lambda ref, *index: ref[index].astype(jnp.float32)
+    mates, fars, nears = [], [], []
+    for piece in range(PIECES):
+        rows, _, _ = piece_rows(piece, row_count)
+        block = left[:, rows, :].reshape(-1, depth)
+        product = lax.dot_general(
+            block, right[...], (((1,), (1 if transposed else 0,)), ((), ())),
+            preferred_element_type=jnp.float32,
+        )
+        part[:, :, rows, :] = product.astype(jnp.bfloat16).reshape(-1, 2, span, width)
+        if piece == 0:
+            greet([{"rep": mate}, {"rep": across}, {"rep": along}])
+        mates.append(
+            remote(part.at[:, 1 - core, rows, :], from_mate.at[:, rows, :], sems, 0, piece, mate)
+        )
+    for piece in range(PIECES):
+        rows, upper, lower = piece_rows(piece, row_count)
+        mates[piece].wait_recv()
+        total = wide(part, far_chip, core, rows) + wide(from_mate, far_chip, rows)
+        send_far[rows, :] = total.astype(jnp.bfloat16)
+        fars.append([
+            remote(send_far.at[upper], far_across.at[piece], sems, 1, piece, across),
+            remote(send_far.at[lower], far_along.at[piece], sems, 2, piece, along),
+        ])
+    for piece in range(PIECES):
+        rows, upper, lower = piece_rows(piece, row_count)
+        fars[piece][0].wait_recv()
+        total = wide(part, along_chip, core, upper) + wide(from_mate, along_chip, upper) + wide(far_across, piece)
+        send_along[upper, :] = total.astype(jnp.bfloat16)
+        total = wide(part, along_chip, core, lower) + wide(from_mate, along_chip, lower)
+        send_along[lower, :] = total.astype(jnp.bfloat16)
+        to_along = remote(send_along.at[rows], got_along.at[rows], sems, 4, piece, along)
+        fars[piece][1].wait_recv()
+        total = wide(part, across_chip, core, lower) + wide(from_mate, across_chip, lower) + wide(far_along, piece)
+        send_across[lower, :] = total.astype(jnp.bfloat16)
+        total = wide(part, across_chip, core, upper) + wide(from_mate, across_chip, upper)
+        send_across[upper, :] = total.astype(jnp.bfloat16)
+        to_across = remote(send_across.at[rows], got_across.at[rows], sems, 3, piece, across)
+        nears.append([to_across, to_along])
+    results = []
+    for piece in range(PIECES):
+        rows, _, _ = piece_rows(piece, row_count)
+        nears[piece][0].wait_recv()
+        nears[piece][1].wait_recv()
+        total = (
+            wide(part, chip, core, rows) + wide(from_mate, chip, rows)
+            + wide(got_across, rows) + wide(got_along, rows)
+        )
+        results.append(finish(piece, rows, total))
+    for piece in range(PIECES):
+        for copy in [mates[piece]] + fars[piece] + nears[piece]:
+            copy.wait_send()
+    return results
+
+
+def scatter_scratch(row_count, width):
+    half = row_count // PIECES // 2
+    return [
+        pltpu.VMEM((4, 2, row_count, width), jnp.bfloat16),
+        pltpu.VMEM((4, row_count, width), jnp.bfloat16),
+        pltpu.VMEM((row_count, width), jnp.bfloat16),
+        pltpu.VMEM((row_count, width), jnp.bfloat16),
+        pltpu.VMEM((row_count, width), jnp.bfloat16),
+        pltpu.VMEM((PIECES, half, width), jnp.bfloat16),
+        pltpu.VMEM((PIECES, half, width), jnp.bfloat16),
+        pltpu.VMEM((row_count, width), jnp.bfloat16),
+        pltpu.VMEM((row_count, width), jnp.bfloat16),
+        pltpu.SemaphoreType.DMA((13, PIECES)),
+        pltpu.SemaphoreType.DMA((13, PIECES)),
+    ]
+
+
+def norm_scale(stream):
+    return lax.rsqrt(jnp.mean(stream * stream, axis=-1, keepdims=True) + epsilon)
+
+
+def forward_exchange(normed, left, right, stream, gain, full, middle, *scratch):
+    sems = scratch[-2:]
+    row_count = stream.shape[0]
+
+    def finish(piece, rows, total):
+        place = lax.axis_index("rep")
+        stepped = stream[rows, :] + total
+        middle[rows, :] = stepped
+        if normed:
+            stepped = stepped * norm_scale(stepped) * gain[...]
+        full[place, rows, :] = stepped.astype(jnp.bfloat16)
+        return gather_send(full, sems, 5, piece, row_count)
+
+    sent = scatter_stage(left, right, False, *scratch[:-2], sems, finish)
+    gather_finish(full, sems, 5, row_count, sent)
+
+
+def backward_exchange(spread, left, right, grad, stream, gain, *rest):
+    if spread:
+        full, stepped_ref, gain_grad = rest[:3]
+        scratch = rest[3:]
+    else:
+        stepped_ref, gain_grad = rest[:2]
+        scratch = rest[2:]
+    sems = scratch[-2:]
+    row_count = stream.shape[0]
+
+    def finish(piece, rows, total):
+        place = lax.axis_index("rep")
+        held = stream[rows, :]
+        scale = norm_scale(held)
+        weighted = total * gain[...]
+        stepped = (
+            grad[rows, :] + scale * weighted
+            - held * (scale * scale * scale) * jnp.mean(weighted * held, axis=-1, keepdims=True)
+        )
+        share = jnp.sum(total * held * scale, axis=0, keepdims=True)
+        gain_grad[...] = share if piece == 0 else gain_grad[...] + share
+        stepped_ref[rows, :] = stepped.astype(stepped_ref.dtype)
+        if not spread:
+            return None
+        full[place, rows, :] = stepped.astype(jnp.bfloat16)
+        return gather_send(full, sems, 5, piece, row_count)
+
+    sent = scatter_stage(left, right, True, *scratch[:-2], sems, finish)
+    if spread:
+        gather_finish(full, sems, 5, row_count, sent)
+
+
+def vmem_specs(count):
+    return [pl.BlockSpec(memory_space=pltpu.VMEM)] * count
+
+
+def comm_params(number):
+    return pltpu.CompilerParams(
+        collective_id=number, has_side_effects=True, vmem_limit_bytes=48 * 1024 * 1024
+    )
+
+
+def run_forward_exchange(number, normed, left, right, stream, gain):
+    row_count, width = stream.shape
+    return pl.pallas_call(
+        functools.partial(forward_exchange, normed),
+        out_shape=(
+            jax.ShapeDtypeStruct((8, row_count, width), jnp.bfloat16),
+            jax.ShapeDtypeStruct((row_count, width), jnp.float32),
+        ),
+        in_specs=vmem_specs(4),
+        out_specs=tuple(vmem_specs(2)),
+        scratch_shapes=scatter_scratch(row_count, width),
+        compiler_params=comm_params(number),
+        name="fwd_exchange_%d" % number,
+    )(left, right, stream, gain)
+
+
+def run_backward_exchange(number, spread, left, right, grad, stream, gain):
+    row_count, width = stream.shape
+    own = (
+        jax.ShapeDtypeStruct((row_count, width), jnp.float32 if spread else jnp.bfloat16),
+        jax.ShapeDtypeStruct((1, width), jnp.float32),
+    )
+    full = (jax.ShapeDtypeStruct((8, row_count, width), jnp.bfloat16),) if spread else ()
+    return pl.pallas_call(
+        functools.partial(backward_exchange, spread),
+        out_shape=full + own,
+        in_specs=vmem_specs(5),
+        out_specs=tuple(vmem_specs(len(full + own))),
+        scratch_shapes=scatter_scratch(row_count, width),
+        compiler_params=comm_params(number),
+        name="bwd_exchange_%d" % number,
+    )(left, right, grad, stream, gain)
+
+
+def opening(tokens, cotangent, gains, full_tokens, full_cotangent, full_gains,
+            send_sem, recv_sem, send_two, recv_two, gain_send, gain_recv):
+    place, mate, across, along = plane_neighbours()
+    plane = lax.axis_index("shard")
+    planes = lax.axis_size("shard")
+    row_count = tokens.shape[0]
+    others = [(plane + step) % planes for step in range(1, planes)]
+    full_tokens[place] = tokens[...]
+    full_cotangent[place] = cotangent[...]
+    full_gains[plane] = gains[...]
+    greet([{"rep": mate}, {"rep": across}, {"rep": along}] + [{"shard": other} for other in others])
+    sent = [gather_send(full_tokens, (send_sem, recv_sem), 0, piece, row_count) for piece in range(PIECES)]
+    gain_copies = []
+    for step in range(1, planes):
+        copy = pltpu.make_async_remote_copy(
+            src_ref=full_gains.at[plane],
+            dst_ref=full_gains.at[plane],
+            send_sem=gain_send.at[step],
+            recv_sem=gain_recv.at[step],
+            device_id={"shard": others[step - 1]},
+            device_id_type=MESH,
+        )
+        copy.start()
+        gain_copies.append(copy)
+    gather_finish(full_tokens, (send_sem, recv_sem), 0, row_count, sent)
+    sent = [gather_send(full_cotangent, (send_two, recv_two), 0, piece, row_count) for piece in range(PIECES)]
+    gather_finish(full_cotangent, (send_two, recv_two), 0, row_count, sent)
+    for copy in gain_copies:
+        copy.wait_recv()
+        copy.wait_send()
+
+
+def run_opening(number, tokens, cotangent, gains):
+    row_count, width = tokens.shape
+    planes = lax.axis_size("shard")
+    full = jax.ShapeDtypeStruct((8, row_count, width), jnp.bfloat16)
+    return pl.pallas_call(
+        opening,
+        out_shape=(full, full, jax.ShapeDtypeStruct((planes,) + gains.shape, gains.dtype)),
+        in_specs=vmem_specs(3),
+        out_specs=tuple(vmem_specs(3)),
+        scratch_shapes=[pltpu.SemaphoreType.DMA((8, PIECES))] * 4
+        + [pltpu.SemaphoreType.DMA((planes,))] * 2,
+        compiler_params=comm_params(number),
+        name="opening",
+    )(tokens, cotangent, gains)
+
+
+def plane_scores(queries, keys_rot, mask):
+    scores = jnp.einsum(
+        "sqhd,std->shqt", queries, keys_rot, preferred_element_type=jnp.float32
+    ) * HEAD ** (-0.5)
+    return jnp.where(mask, scores, masked_score)
+
+
+def plane_attention(normed, weights, mask, cosine, sine):
+    blocks, row_count, width = normed.shape
+    heads = HEADS // blocks
+    split = heads * HEAD
+    mixed_in = left_product(normed.reshape(-1, width), weights).reshape(blocks, row_count, -1)
+    queries = mixed_in[..., :split].reshape(blocks, row_count, heads, HEAD)
+    queries = rotate(queries, cosine, sine).astype(jnp.bfloat16)
+    keys_rot = rotate(mixed_in[..., split:split + HEAD], cosine[:, 0], sine[:, 0]).astype(jnp.bfloat16)
+    values = mixed_in[..., split + HEAD:].astype(jnp.bfloat16)
+    scores = plane_scores(queries, keys_rot, mask)
+    row_max = jnp.max(scores, axis=-1, keepdims=True)
+    shifted = jnp.exp(scores - row_max)
+    row_total = jnp.sum(shifted, axis=-1, keepdims=True)
+    attention = shifted / row_total
+    log_total = row_max + jnp.log(row_total)
+    mixed = jnp.einsum(
+        "shqt,std->sqhd", attention.astype(jnp.bfloat16), values, preferred_element_type=jnp.float32
+    )
+    mixed = mixed.reshape(blocks, row_count, split).astype(jnp.bfloat16)
+    return (mixed, (queries, keys_rot, values, log_total, mixed))
+
+
+def plane_attention_back(mixed_grad, kept, mask, cosine, sine):
+    queries, keys_rot, values, log_total, _ = kept
+    blocks, row_count, heads, _ = queries.shape
+    mixed_grad = mixed_grad.reshape(queries.shape)
+    scores = plane_scores(queries, keys_rot, mask)
+    attention = jnp.exp(scores - log_total)
+    attention_grad = jnp.einsum("sqhd,std->shqt", mixed_grad, values, preferred_element_type=jnp.float32)
+    value_grad = jnp.einsum(
+        "shqt,sqhd->std", attention.astype(jnp.bfloat16), mixed_grad, preferred_element_type=jnp.float32
+    ).astype(jnp.bfloat16)
+    row_dot = jnp.sum(attention * attention_grad, axis=-1, keepdims=True)
+    score_grad = (attention * (attention_grad - row_dot)).astype(jnp.bfloat16)
+    query_grad = jnp.einsum(
+        "shqt,std->sqhd", score_grad, keys_rot, preferred_element_type=jnp.float32
+    ) * HEAD ** (-0.5)
+    key_grad = jnp.einsum(
+        "shqt,sqhd->std", score_grad, queries, preferred_element_type=jnp.float32
+    ) * HEAD ** (-0.5)
+    query_grad = unrotate(query_grad, cosine, sine).astype(jnp.bfloat16)
+    key_grad = unrotate(key_grad, cosine[:, 0], sine[:, 0]).astype(jnp.bfloat16)
+    return jnp.concatenate([query_grad.reshape(blocks, row_count, -1), key_grad, value_grad], axis=-1)
+
+
+def plane_shards(
+    tokens,
+    cotangent,
+    lengths,
+    deal_order,
+    attention_gain,
+    query_weight,
+    key_weight,
+    value_weight,
+    output_weight,
+    feedforward_gain,
+    gate_weight,
+    up_weight,
+    down_weight,
+):
+    place, plane = lax.axis_index("rep"), lax.axis_index("shard")
+    places, planes = lax.axis_size("rep"), lax.axis_size("shard")
+    row_count, width = tokens.shape[1:]
+    share = width // planes
+    heads = HEADS // places
+    split = heads * HEAD
+    hidden = gate_weight.shape[2]
+    unit = hidden // places // planes
+    head_plane = places // planes
+
+    def head_columns(weight, layer, size):
+        return lax.dynamic_slice_in_dim(weight[layer], place * size, size, 1)
+
+    def unit_columns(weight, layer):
+        parted = weight[layer].reshape(share, planes, places, unit)
+        return lax.dynamic_index_in_dim(parted, place, 2, keepdims=False).reshape(share, planes * unit)
+
+    def over_planes(piece):
+        return lax.all_gather(piece, "shard", axis=0, tiled=True)
+
+    def head_rows(layer):
+        rows = lax.dynamic_slice_in_dim(
+            output_weight[layer], (place % head_plane) * split, split, 0
+        )
+        arrived = jnp.where(plane == place // head_plane, rows, jnp.zeros_like(rows))
+        for step in range(1, planes):
+            pairs = [
+                (spot * planes + spot // head_plane, spot * planes + (spot // head_plane + step) % planes)
+                for spot in range(places)
+            ]
+            arrived = arrived + lax.ppermute(rows, ("rep", "shard"), pairs)
+        return arrived
+
+    projections, outputs, openers, downs = [], [], [], []
+    for layer in range(LAYERS):
+        projections.append(over_planes(jnp.concatenate(
+            [head_columns(query_weight, layer, split), head_columns(key_weight, layer, HEAD),
+             head_columns(value_weight, layer, HEAD)], axis=1)))
+        outputs.append(head_rows(layer))
+        openers.append(over_planes(jnp.concatenate(
+            [unit_columns(gate_weight, layer), unit_columns(up_weight, layer)], axis=1)))
+        downs.append(over_planes(lax.dynamic_slice_in_dim(down_weight[layer], place * unit, unit, 0)))
+
+    gains = jnp.concatenate([attention_gain, feedforward_gain] * 2, axis=0).astype(jnp.float32)
+    full_tokens, full_cotangent, full_gains = run_opening(0, tokens[0], cotangent[0], gains)
+    full_gains = full_gains.transpose(1, 0, 2).reshape(-1, width)
+    attend_gain = [full_gains[layer][None] for layer in range(LAYERS)]
+    forward_gain = [full_gains[LAYERS + layer][None] for layer in range(LAYERS)]
+
+    position = jnp.arange(row_count)
+    spots = jnp.arange(places)
+    plane_lengths = lengths[spots * planes + plane]
+    valid = position[None, :] < plane_lengths[:, None]
+    mask = (position[None, :] <= position[:, None])[None] & valid[:, None, :]
+    mask = mask[:, None]
+    cosine, sine = rope_tables(row_count)
+    wanted = deal_order[spots * planes + plane] // planes
+    inverse = jnp.sum(jnp.where(wanted[None, :] == spots[:, None], spots[None, :], 0), axis=1)
+    branch_full = jnp.where(valid[:, :, None], full_cotangent[inverse], jnp.zeros((), jnp.bfloat16))
+    own_valid = lax.dynamic_index_in_dim(valid, place, 0, keepdims=False)[:, None]
+    grad = lax.dynamic_index_in_dim(branch_full, place, 0, keepdims=False).astype(jnp.float32)
+
+    stream = tokens[0].astype(jnp.float32)
+    wide = full_tokens.astype(jnp.float32)
+    normed = (wide * norm_scale(wide) * attend_gain[0]).astype(jnp.bfloat16)
+    kept = []
+    ended = None
+    for layer in range(LAYERS):
+        mixed, attended = plane_attention(normed, projections[layer], mask, cosine, sine)
+        normed_two, middle = run_forward_exchange(1, True, mixed, outputs[layer], stream, forward_gain[layer])
+        both = left_product(normed_two.reshape(-1, width), openers[layer])
+        gate_lin, up_lin = jnp.split(both.reshape(places, row_count, -1), 2, axis=-1)
+        active = (gate_lin * jax.nn.sigmoid(gate_lin) * up_lin).astype(jnp.bfloat16)
+        kept.append((stream, normed, attended, middle, normed_two, gate_lin, up_lin, active))
+        if layer + 1 < LAYERS:
+            normed, stream = run_forward_exchange(2, True, active, downs[layer], middle, attend_gain[layer + 1])
+        else:
+            ended, _ = run_forward_exchange(3, False, active, downs[layer], middle, attend_gain[layer])
+    chosen = lax.dynamic_index_in_dim(wanted, place, 0, keepdims=False)
+    chosen_valid = lax.dynamic_index_in_dim(valid, chosen, 0, keepdims=False)[:, None]
+    layer_output = jnp.where(
+        chosen_valid, lax.dynamic_index_in_dim(ended, chosen, 0, keepdims=False), jnp.zeros((), jnp.bfloat16)
+    )[None]
+
+    def summed(partial):
+        return lax.psum_scatter(partial.astype(jnp.bfloat16), "shard", scatter_dimension=0, tiled=True)
+
+    def over_places(piece):
+        return lax.all_gather(piece, "rep", axis=0, tiled=False)
+
+    def back_columns(gathered, parts):
+        return gathered.reshape(places, share, parts, -1).transpose(1, 2, 0, 3).reshape(share, -1).astype(jnp.float32)
+
+    layer_grads = [None] * LAYERS
+    gain_parts = [None] * (2 * LAYERS)
+    for layer in reversed(range(LAYERS)):
+        stream, normed, attended, middle, normed_two, gate_lin, up_lin, active = kept[layer]
+        flat = branch_full.reshape(-1, width)
+        active_grad = right_transposed(flat, downs[layer]).reshape(active.shape)
+        down_share = summed(row_sum_product(active.reshape(-1, active.shape[-1]), flat))
+        sigma = jax.nn.sigmoid(gate_lin)
+        gate_grad = (active_grad * up_lin * sigma * (1.0 + gate_lin * (1.0 - sigma))).astype(jnp.bfloat16)
+        up_grad = (active_grad * gate_lin * sigma).astype(jnp.bfloat16)
+        both_grad = jnp.concatenate([gate_grad, up_grad], axis=-1)
+        opener_share = summed(row_sum_product(normed_two.reshape(-1, width), both_grad.reshape(places * row_count, -1)))
+        branch_full, grad, gain_parts[LAYERS + layer] = run_backward_exchange(
+            4, True, both_grad, openers[layer], grad, middle, forward_gain[layer])
+        flat = branch_full.reshape(-1, width)
+        mixed_grad = right_transposed(flat, outputs[layer]).astype(jnp.bfloat16)
+        mixed = attended[-1]
+        output_share = lax.psum(row_sum_product(mixed.reshape(-1, split), flat).astype(jnp.bfloat16), "shard")
+        joint_grad = plane_attention_back(mixed_grad, attended, mask, cosine, sine)
+        projection_share = summed(row_sum_product(normed.reshape(-1, width), joint_grad.reshape(places * row_count, -1)))
+        if layer > 0:
+            branch_full, grad, gain_parts[layer] = run_backward_exchange(
+                5, True, joint_grad, projections[layer], grad, stream, attend_gain[layer])
+        else:
+            input_grad, gain_parts[layer] = run_backward_exchange(
+                6, False, joint_grad, projections[layer], grad, stream, attend_gain[layer])
+        down_grad = over_places(down_share).reshape(places * unit, width).astype(jnp.float32)
+        opener_full = over_places(opener_share)
+        gate_weight_grad = back_columns(opener_full[..., :planes * unit], planes)
+        up_weight_grad = back_columns(opener_full[..., planes * unit:], planes)
+        output_full = over_places(output_share).reshape(places * split, width)
+        output_grad = lax.dynamic_slice_in_dim(output_full, plane * share, share, 0).astype(jnp.float32)
+        projection_full = over_places(projection_share)
+        query_grad = back_columns(projection_full[..., :split], 1)
+        key_grad = back_columns(projection_full[..., split:split + HEAD], 1)
+        value_grad = back_columns(projection_full[..., split + HEAD:], 1)
+        layer_grads[layer] = (query_grad, key_grad, value_grad, output_grad, gate_weight_grad, up_weight_grad, down_grad)
+
+    gain_sum = lax.psum(jnp.concatenate(gain_parts, axis=0), ("rep", "shard"))
+    gain_sum = lax.dynamic_slice_in_dim(gain_sum, plane * share, share, 1)
+    stacked = [jnp.stack([layer_grads[layer][member] for layer in range(LAYERS)]) for member in range(7)]
+    return (
+        layer_output,
+        input_grad[None],
+        gain_sum[:LAYERS],
+        stacked[0],
+        stacked[1],
+        stacked[2],
+        stacked[3],
+        gain_sum[LAYERS:],
+        stacked[4],
+        stacked[5],
+        stacked[6],
+    )
+
+
 def solution(mesh):
     placed = (
         P(("rep", "shard"), None, None),
@@ -380,8 +905,9 @@
         P(None, "shard", None),
         P(None, "shard", None),
     )
+    split_heads = mesh.shape["rep"] == KV_HEADS and mesh.shape["rep"] % mesh.shape["shard"] == 0
     return jax.shard_map(
-        shards,
+        plane_shards if split_heads else whole_weight_shards,
         mesh=mesh,
         in_specs=placed,
         out_specs=(

time: 4240 us -> 1270 us (0.30)
  waiting for transfers between devices: 3760 us -> 417 us
  Pallas kernels: 0 us -> 380 us
  local copies, waits for them, and re-layouts: 57.7 us -> 216 us
  matrix products: 228 us -> 95.3 us
    all_gather x16 -> x14, waiting for transfers between devices: 1730 us -> 130 us  [the longest x8 130 us: over_places(): return lax.all_gather(piece, 'rep', axis=0, tiled=False)]
    reduce_scatter x14 -> x6, waiting for transfers between devices: 1730 us -> 223 us  [summed(): lax.psum_scatter(partial.astype(jnp.bfloat16), 'shard', scatter_dimension...]
    pallas_call x0 -> x9, Pallas kernels: none -> 380 us  [the longest x4 142 us: run_forward_exchange(): pl.pallas_call(functools.partial(forward_exchange, normed), out_shape=(ja...]
    psum x1, waiting for transfers between devices: 305 us -> 57.3 us  [plane_shards(): lax.psum(row_sum_product(mixed.reshape(-1, split), flat).astype(jnp.bfloa...]
    convert_element_type x4 -> x16, local copies, waits for them, and re-layouts: 1.41 us -> 79.1 us  [the longest x12 74.3 us: back_columns(): gathered.reshape(places, share, parts, -1).transpose(1, 2, 0, 3)]
    dot_general x14 -> x4, matrix products: 76.6 us -> 19.6 us  [right_transposed(): jnp.einsum('lf,df->ld', grad_rows, weight, preferred_element_type=jnp.flo...]
    dot_general x14 -> x4, matrix products: 74.3 us -> 23.1 us  [left_product(): return jnp.dot(left, right, preferred_element_type=jnp.float32)]
    all_gather x4 -> x0, blocking collectives: 50.8 us -> none  [the longest x2 26.9 us: gather_forward(): lax.all_gather(stacked[5][layer_index], 'shard', axis=0, tiled=True)]
  transfers between devices with their start and end apart: 31 -> 27, of which waited for: 27 -> 11; matrix products, arithmetic and copies ran while one was open for 6% -> 17% of each run, Pallas kernels for 0% -> 21%
where the time goes in v1:
time: 1270 us; the launch traced here: 1260 us
  waiting for transfers between devices  417 us (33%)
  Pallas kernels  380 us (30%)
  local copies, waits for them, and re-layouts  216 us (17%)
  matrix products  95.3 us (8%)
  other arithmetic  69.2 us (5%)
  blocking collectives  40.2 us (3%)
  starting transfers between devices  23.8 us (2%)
  between operations  18.1 us (1%)
    reduce_scatter x6, waiting for transfers between devices, summed(): lax.psum_scatter(partial.astype(jnp.bfloat16), 'shard', scatter_dimension...  223 us
    pallas_call x4, Pallas kernels, run_forward_exchange(): pl.pallas_call(functools.partial(forward_exchange, normed), out_shape=(ja...  142 us
    pallas_call x4, Pallas kernels, run_backward_exchange(): pl.pallas_call(functools.partial(backward_exchange, spread), out_shape=fu...  136 us
    all_gather x8, waiting for transfers between devices, over_places(): return lax.all_gather(piece, 'rep', axis=0, tiled=False)  130 us
    pallas_call x1, Pallas kernels, run_opening(): pl.pallas_call(opening, out_shape=(full, full, jax.ShapeDtypeStruct((plan...  102 us
    convert_element_type x12, local copies, waits for them, and re-layouts, back_columns(): gathered.reshape(places, share, parts, -1).transpose(1, 2, 0, 3)  74.3 us
    unnamed x210, local copies, waits for them, and re-layouts  58.4 us
    psum x1, waiting for transfers between devices, plane_shards(): lax.psum(row_sum_product(mixed.reshape(-1, split), flat).astype(jnp.bfloa...  57.3 us
  transfers between devices with their start and end apart: 27, of which 11 were waited for; matrix products, arithmetic and copies ran while one was open for 17% of the time, Pallas kernels for 21%

profile of v1, /device:TPU:0, one launch (start us, length us, event | category | flops | bytes accessed | tf_op | source)
XLA Modules:
  0.0 1259.9 jit_solution(1447642528003763981)
XLA Ops:
  29.1 8.0 dynamic-slice_reduce_fusion.2
  81.5 102.3 %opening.1 = (bf16[8,128,1536]{2,1,0:T(8,128)(2,1)S(1)}, bf16[8,128,1536]{2,1,0:T(8,128)(2,1)}, f32[4,8,384]{2,1,0:T(8,128)S(1)}) custom-call(bf16[128,1536]{1,0:T(8,128)(2,1)S(1)} %bitcast.327, bf16[128,1536]{1,0:T(8,128)(2,1)S(1)} %bitcast.328, f32[8,384]{1,0:T(8,128)S(1)} %maximum_convert_fusion.7.gains), custom_call_target="tpu_custom_call" | custom-call | tf_op jit(solution)/shard_map/opening/pallas_call | solution.py:664
  195.8 7.5 collective-permute-start.5
  231.2 32.2 %fwd_exchange_1.2 = (bf16[8,128,1536]{2,1,0:T(8,128)(2,1)S(1)}, f32[128,1536]{1,0:T(8,128)S(1)}) custom-call(bf16[8,128,192]{2,1,0:T(8,128)(2,1)S(1)} %copy.269.left, bf16[192,1536]{1,0:T(8,128)(2,1)S(1)} %add_add_fusion.1.right, f32[128,1536]{1,0:T(8,128)S(1)} %bitcast_convert_fusion.3.stream, f32[1,1536]{1,0:T(1,128)S(1)} %bitcast.333), custom_call_target="tpu_custom_call" | custom-call | tf_op jit(solution)/shard_map/fwd_exchange_1/pallas_call | solution.py:596
  275.7 34.1 %fwd_exchange_2.1 = (bf16[8,128,1536]{2,1,0:T(8,128)(2,1)}, f32[128,1536]{1,0:T(8,128)S(1)}) custom-call(bf16[8,128,512]{2,1,0:T(8,128)(2,1)S(1)} %multiply_convert_fusion.5.left, bf16[512,1536]{1,0:T(8,128)(2,1)S(1)} %bitcast.326, f32[128,1536]{1,0:T(8,128)S(1)} %get-tuple-element.35.stream, f32[1,1536]{1,0:T(1,128)S(1)} %bitcast.330), custom_call_target="tpu_custom_call" | custom-call | tf_op jit(solution)/shard_map/fwd_exchange_2/pallas_call | solution.py:596
  326.2 32.3 %fwd_exchange_1.3 = (bf16[8,128,1536]{2,1,0:T(8,128)(2,1)S(1)}, f32[128,1536]{1,0:T(8,128)S(1)}) custom-call(bf16[8,128,192]{2,1,0:T(8,128)(2,1)S(1)} %copy-done.13, bf16[192,1536]{1,0:T(8,128)(2,1)S(1)} %copy-done.11, f32[128,1536]{1,0:T(8,128)S(1)} %get-tuple-element.37.stream, f32[1,1536]{1,0:T(1,128)S(1)} %bitcast.335), custom_call_target="tpu_custom_call" | custom-call | tf_op jit(solution)/shard_map/fwd_exchange_1/pallas_call | solution.py:596
  360.2 8.5 fusion.3
  368.8 7.3 multiply_convert_fusion.3
  377.7 38.0 %bwd_exchange_4.2 = (bf16[8,128,1536]{2,1,0:T(8,128)(2,1)}, f32[128,1536]{1,0:T(8,128)S(1)}, f32[1,1536]{1,0:T(1,128)S(1)}) custom-call(bf16[8,128,1024]{2,1,0:T(8,128)(2,1)S(1)} %pad_maximum_fusion.left, bf16[1536,1024]{1,0:T(8,128)(2,1)} %all-gather.29.cloned.1.call-done.right, f32[128,1536]{1,0:T(8,128)S(1)} %copy-done.6, ...), custom_call_target="tpu_custom_call" | custom-call | tf_op jit(solution)/shard_map/bwd_exchange_4/pallas_call | solution.py:617
  435.4 34.3 %bwd_exchange_5.1 = (bf16[8,128,1536]{2,1,0:T(8,128)(2,1)}, f32[128,1536]{1,0:T(8,128)S(1)}, f32[1,1536]{1,0:T(1,128)S(1)}) custom-call(bf16[8,128,384]{2,1,0:T(8,128)(2,1)S(1)} %pad_maximum_fusion.4.left, bf16[1536,384]{1,0:T(8,128)(2,1)S(1)} %copy-done.19, f32[128,1536]{1,0:T(8,128)S(1)} %copy-done.24, f32[128,1536]{1,0:T(8,128)S(1)} %get-tuple-element.37.stream, ...), custom_call_target="tpu_custom_call" | custom-call | tf_op jit(solution)/shard_map/bwd_exchange_5/pallas_call | solution.py:617
  477.2 38.3 %bwd_exchange_4.3 = (bf16[8,128,1536]{2,1,0:T(8,128)(2,1)}, f32[128,1536]{1,0:T(8,128)S(1)}, f32[1,1536]{1,0:T(1,128)S(1)}) custom-call(bf16[8,128,1024]{2,1,0:T(8,128)(2,1)S(1)} %pad_maximum_fusion.1.left, bf16[1536,1024]{1,0:T(8,128)(2,1)} %all-gather.25.cloned.1.call-done.right, f32[128,1536]{1,0:T(8,128)S(1)} %get-tuple-element.45.grad, ...), custom_call_target="tpu_custom_call" | custom-call | tf_op jit(solution)/shard_map/bwd_exchange_4/pallas_call | solution.py:617
  558.2 7.3 bitcast_convert_fusion
  566.8 7.3 bitcast_convert_fusion.1
  574.7 23.9 %reduce-scatter.9.cloned.1.call-done = bf16[384,384]{1,0:T(8,128)(2,1)} async-done(((bf16[1536,384]{1,0:T(8,128)(2,1)}), bf16[384,384]{1,0:T(8,128)(2,1)}) %reduce-scatter.9.cloned.1.call-update) | async-done | bytes 294928 | tf_op jit(solution)/shard_map/reduce_scatter | solution.py:828
  598.7 36.9 %reduce-scatter.17.cloned.1.call-done = bf16[128,1536]{1,0:T(8,128)(2,1)} async-done(((bf16[512,1536]{1,0:T(8,128)(2,1)}), bf16[128,1536]{1,0:T(8,128)(2,1)}) %reduce-scatter.17.cloned.1.call-update) | async-done | bytes 393232 | tf_op jit(solution)/shard_map/reduce_scatter | solution.py:828
  635.6 37.0 %reduce-scatter.15.cloned.1.call-done = bf16[128,1536]{1,0:T(8,128)(2,1)} async-done(((bf16[512,1536]{1,0:T(8,128)(2,1)}), bf16[128,1536]{1,0:T(8,128)(2,1)}) %reduce-scatter.15.cloned.1.call-update) | async-done | bytes 393232 | tf_op jit(solution)/shard_map/reduce_scatter | solution.py:828
  672.7 57.3 %all-reduce.3.cloned.1.call-done = (bf16[1,192,1536]{2,1,0:T(8,128)(2,1)}, bf16[1,192,1536]{2,1,0:T(8,128)(2,1)}) async-done(((bf16[1,192,1536]{2,1,0:T(8,128)(2,1)}, bf16[1,192,1536]{2,1,0:T(8,128)(2,1)}), (bf16[1,192,1536]{2,1,0:T(8,128)(2,1)}, bf16[1,192,1536]{2,1,0:T(8,128)(2,1)})) %all-reduce.3.cloned.1.call-update) | async-done | bytes 1179664 | tf_op jit(solution)/shard_map/psum | solution.py:853
  730.7 61.8 %reduce-scatter.13.cloned.1.call-done = bf16[384,1024]{1,0:T(8,128)(2,1)} async-done(((bf16[1536,1024]{1,0:T(8,128)(2,1)}), bf16[384,1024]{1,0:T(8,128)(2,1)}) %reduce-scatter.13.cloned.1.call-update) | async-done | bytes 786448 | tf_op jit(solution)/shard_map/reduce_scatter | solution.py:828
  792.6 63.1 %reduce-scatter.11.cloned.1.call-done = bf16[384,1024]{1,0:T(8,128)(2,1)} async-done(((bf16[1536,1024]{1,0:T(8,128)(2,1)}), bf16[384,1024]{1,0:T(8,128)(2,1)}) %reduce-scatter.11.cloned.1.call-update) | async-done | bytes 786448 | tf_op jit(solution)/shard_map/reduce_scatter | solution.py:828
  862.8 43.5 %fwd_exchange_3.1 = (bf16[8,128,1536]{2,1,0:T(8,128)(2,1)}, f32[128,1536]{1,0:T(8,128)}) custom-call(bf16[8,128,512]{2,1,0:T(8,128)(2,1)S(1)} %copy-done.20, bf16[512,1536]{1,0:T(8,128)(2,1)S(1)} %bitcast.325, f32[128,1536]{1,0:T(8,128)S(1)} %copy-done.5, f32[1,1536]{1,0:T(1,128)S(1)} %bitcast.332), custom_call_target="tpu_custom_call" | custom-call | tf_op jit(solution)/shard_map/fwd_exchange_3/pallas_call | solution.py:596
  906.3 25.4 %bwd_exchange_6.1 = (bf16[128,1536]{1,0:T(8,128)(2,1)S(1)}, f32[1,1536]{1,0:T(1,128)S(1)}) custom-call(bf16[8,128,384]{2,1,0:T(8,128)(2,1)S(1)} %pad_maximum_fusion.5.left, bf16[1536,384]{1,0:T(8,128)(2,1)S(1)} %copy-done.18, f32[128,1536]{1,0:T(8,128)S(1)} %copy-done.22, f32[128,1536]{1,0:T(8,128)S(1)} %bitcast_convert_fusion.3.stream, f32[1,1536]{1,0:T(1,128)S(1)} %bitcast.337), custom_call_target="tpu_custom_call" | custom-call | tf_op jit(solution)/shard_map/bwd_exchange_6/pallas_call | solution.py:617
  931.7 40.2 %psum.21 = f32[4,1536]{1,0:T(4,128)S(1)} all-reduce(f32[4,1536]{1,0:T(4,128)S(1)} %pad_maximum_fusion.9), channel_id=1, replica_groups=mesh['rep'=8,'shard'=4] {'rep','shard'}, use_global_device_ids=true, to_apply=%region_8.9 | all-reduce | flops 6144 | bytes 49152 | tf_op jit(solution)/shard_map/psum | solution.py:874
  1007.1 8.8 maximum_convert_fusion.2
  1015.9 25.0 %all-gather.33.cloned.1.call-done = bf16[8,192,1536]{2,1,0:T(8,128)(2,1)} async-done(((bf16[1,192,1536]{2,1,0:T(8,128)(2,1)}), bf16[8,192,1536]{2,1,0:T(8,128)(2,1)}) %all-gather.33.cloned.1.call-update) | async-done | bytes 4718608 | tf_op jit(solution)/shard_map/all_gather | solution.py:831
  1042.3 39.3 %all-gather.31.cloned.1.call-done = bf16[8,192,1536]{2,1,0:T(8,128)(2,1)} async-done(((bf16[1,192,1536]{2,1,0:T(8,128)(2,1)}), bf16[8,192,1536]{2,1,0:T(8,128)(2,1)}) %all-gather.31.cloned.1.call-update) | async-done | bytes 4718608 | tf_op jit(solution)/shard_map/all_gather | solution.py:831
  1085.5 43.3 %all-gather.45.cloned.1.call-done = bf16[3072,1024]{1,0:T(8,128)(2,1)} async-done(((bf16[384,1024]{1,0:T(8,128)(2,1)}), bf16[3072,1024]{1,0:T(8,128)(2,1)}) %all-gather.45.cloned.1.call-update) | async-done | bytes 6291472 | tf_op jit(solution)/shard_map/all_gather | solution.py:831
  1140.4 7.2 copy.408
  1153.5 22.6 %all-gather.43.cloned.1.call-done = bf16[3072,1024]{1,0:T(8,128)(2,1)} async-done(((bf16[384,1024]{1,0:T(8,128)(2,1)}), bf16[3072,1024]{1,0:T(8,128)(2,1)}) %all-gather.43.cloned.1.call-update) | async-done | bytes 6291472 | tf_op jit(solution)/shard_map/all_gather | solution.py:831
  1187.7 7.2 copy.409
  1206.2 7.2 copy.411
  1224.9 7.2 copy.410
  1237.9 8.6 maximum_convert_fusion
  (410 shorter events, 319.1 us)
Async XLA Ops:
  7.2 72.2 %copy-start = (s32[32]{0:T(128)S(1)}, s32[32]{0:T(128)}, u32[]{:S(2)}) copy-start(s32[32]{0:T(128)} %param.16) | copy-start | bytes 388
  7.2 209.3 %all-gather.23.cloned.1.call-start = ((), (), s32[]{:S(2)}) async-start(), calls=%async_computation.6 | async-start | bytes 1474560 | tf_op jit(solution)/shard_map/all_gather | solution.py:761
  16.5 248.5 %all-gather.25.cloned.1.call-start = ((), (), s32[]{:S(2)}) async-start(), calls=%async_computation.7 | async-start | bytes 3932160 | tf_op jit(solution)/shard_map/all_gather | solution.py:761
  38.3 236.0 %all-gather.35.cloned.1.call-start = ((), (), s32[]{:S(2)}) async-start(), calls=%async_computation.18 | async-start | bytes 1966080 | tf_op jit(solution)/shard_map/all_gather | solution.py:761
  44.1 265.9 %all-gather.27.cloned.1.call-start = ((), (), s32[]{:S(2)}) async-start(), calls=%async_computation.8 | async-start | bytes 1474560 | tf_op jit(solution)/shard_map/all_gather | solution.py:761
  47.3 313.0 %all-gather.29.cloned.1.call-start = ((), (), s32[]{:S(2)}) async-start(), calls=%async_computation.9 | async-start | bytes 3932160 | tf_op jit(solution)/shard_map/all_gather | solution.py:761
  57.5 311.3 %all-gather.37.cloned.1.call-start = ((), (), s32[]{:S(2)}) async-start(), calls=%async_computation.19 | async-start | bytes 1966080 | tf_op jit(solution)/shard_map/all_gather | solution.py:761
  61.5 134.4 %collective-permute-start.1 = (bf16[192,1536]{1,0:T(8,128)(2,1)}, bf16[192,1536]{1,0:T(8,128)(2,1)}, u32[]{:S(2)}, u32[]{:S(2)}) collective-permute-start(bf16[192,1536]{1,0:T(8,128)(2,1)} %dynamic-slice_bitcast_fusion.3), channel_id=1, source_target_pairs={{0,2},{4,6},{9,11},{13,15},{18,16},{22,20},{27,25},{31,29}} | collective-permute-start | bytes 1769480 | tf_op jit(solution)/shard_map/ppermute | solution.py:773
  68.2 138.3 %collective-permute-start = (bf16[192,1536]{1,0:T(8,128)(2,1)}, bf16[192,1536]{1,0:T(8,128)(2,1)}, u32[]{:S(2)}, u32[]{:S(2)}) collective-permute-start(bf16[192,1536]{1,0:T(8,128)(2,1)} %dynamic-slice_bitcast_fusion.3), channel_id=1, source_target_pairs={{0,1},{4,5},{9,10},{13,14},{18,19},{22,23},{27,24},{31,28}} | collective-permute-start | bytes 1769480 | tf_op jit(solution)/shard_map/ppermute | solution.py:773
  70.3 136.2 %collective-permute-start.2 = (bf16[192,1536]{1,0:T(8,128)(2,1)}, bf16[192,1536]{1,0:T(8,128)(2,1)}, u32[]{:S(2)}, u32[]{:S(2)}) collective-permute-start(bf16[192,1536]{1,0:T(8,128)(2,1)} %dynamic-slice_bitcast_fusion.3), channel_id=1, source_target_pairs={{0,3},{4,7},{9,8},{13,12},{18,17},{22,21},{27,26},{31,30}} | collective-permute-start | bytes 1769480 | tf_op jit(solution)/shard_map/ppermute | solution.py:773
  73.3 135.2 %collective-permute-start.4 = (bf16[192,1536]{1,0:T(8,128)(2,1)}, bf16[192,1536]{1,0:T(8,128)(2,1)}, u32[]{:S(2)}, u32[]{:S(2)}) collective-permute-start(bf16[192,1536]{1,0:T(8,128)(2,1)} %dynamic-slice_bitcast_fusion.2), channel_id=1, source_target_pairs={{0,2},{4,6},{9,11},{13,15},{18,16},{22,20},{27,25},{31,29}} | collective-permute-start | bytes 1769480 | tf_op jit(solution)/shard_map/ppermute | solution.py:773
  75.4 133.1 %collective-permute-start.3 = (bf16[192,1536]{1,0:T(8,128)(2,1)}, bf16[192,1536]{1,0:T(8,128)(2,1)}, u32[]{:S(2)}, u32[]{:S(2)}) collective-permute-start(bf16[192,1536]{1,0:T(8,128)(2,1)} %dynamic-slice_bitcast_fusion.2), channel_id=1, source_target_pairs={{0,1},{4,5},{9,10},{13,14},{18,19},{22,23},{27,24},{31,28}} | collective-permute-start | bytes 1769480 | tf_op jit(solution)/shard_map/ppermute | solution.py:773
  79.3 494.9 %reduce-scatter.7.cloned.1.call-start = ((), (), s32[]{:S(2)}) async-start(), calls=%async_computation.10 | async-start | bytes 1474560 | tf_op jit(solution)/shard_map/reduce_scatter | solution.py:828
  81.4 109.3 %copy-start.87 = (pred[8,128]{1,0:T(8,128)(4,1)}, pred[8,128]{1,0:T(8,128)(4,1)S(1)}, u32[]{:S(2)}) copy-start(pred[8,128]{1,0:T(8,128)(4,1)S(1)} %iota_compare_fusion.2) | copy-start | bytes 3076
  195.8 18.0 %collective-permute-start.5 = (bf16[192,1536]{1,0:T(8,128)(2,1)}, bf16[192,1536]{1,0:T(8,128)(2,1)}, u32[]{:S(2)}, u32[]{:S(2)}) collective-permute-start(bf16[192,1536]{1,0:T(8,128)(2,1)} %dynamic-slice_bitcast_fusion.2), channel_id=1, source_target_pairs={{0,3},{4,7},{9,8},{13,12},{18,17},{22,21},{27,26},{31,30}} | collective-permute-start | bytes 1769480 | tf_op jit(solution)/shard_map/ppermute | solution.py:773
  537.4 61.2 %reduce-scatter.9.cloned.1.call-start = ((), (), s32[]{:S(2)}) async-start(), calls=%async_computation.11 | async-start | bytes 1474560 | tf_op jit(solution)/shard_map/reduce_scatter | solution.py:828
  542.2 93.3 %reduce-scatter.17.cloned.1.call-start = ((), (), s32[]{:S(2)}) async-start(), calls=%async_computation.17 | async-start | bytes 1966080 | tf_op jit(solution)/shard_map/reduce_scatter | solution.py:828
  547.8 124.8 %reduce-scatter.15.cloned.1.call-start = ((), (), s32[]{:S(2)}) async-start(), calls=%async_computation.16 | async-start | bytes 1966080 | tf_op jit(solution)/shard_map/reduce_scatter | solution.py:828
  552.8 177.2 %all-reduce.3.cloned.1.call-start = ((), (), s32[]{:S(2)}) async-start(), calls=%async_computation.26 | async-start | bytes 2359296 | tf_op jit(solution)/shard_map/psum | solution.py:853
  558.1 234.4 %reduce-scatter.13.cloned.1.call-start = ((), (), s32[]{:S(2)}) async-start(), calls=%async_computation.15 | async-start | bytes 3932160 | tf_op jit(solution)/shard_map/reduce_scatter | solution.py:828
  565.5 290.2 %reduce-scatter.11.cloned.1.call-start = ((), (), s32[]{:S(2)}) async-start(), calls=%async_computation.14 | async-start | bytes 3932160 | tf_op jit(solution)/shard_map/reduce_scatter | solution.py:828
  574.1 286.1 %copy-start.5 = (f32[128,1536]{1,0:T(8,128)S(1)}, f32[128,1536]{1,0:T(8,128)}, u32[]{:S(2)}) copy-start(f32[128,1536]{1,0:T(8,128)} %copy-done.4) | copy-start | bytes 2359300
  574.1 400.3 %all-gather.39.cloned.1.call-start = ((), (), s32[]{:S(2)}) async-start(), calls=%async_computation.20 | async-start | bytes 2654208 | tf_op jit(solution)/shard_map/all_gather | solution.py:831
  574.7 407.2 %all-gather.41.cloned.1.call-start = ((), (), s32[]{:S(2)}) async-start(), calls=%async_computation.21 | async-start | bytes 2654208 | tf_op jit(solution)/shard_map/all_gather | solution.py:831
  598.6 408.5 %all-gather.49.cloned.1.call-start = ((), (), s32[]{:S(2)}) async-start(), calls=%async_computation.25 | async-start | bytes 3538944 | tf_op jit(solution)/shard_map/all_gather | solution.py:831
  635.6 371.5 %all-gather.47.cloned.1.call-start = ((), (), s32[]{:S(2)}) async-start(), calls=%async_computation.24 | async-start | bytes 3538944 | tf_op jit(solution)/shard_map/all_gather | solution.py:831
  672.6 233.7 %copy-start.18 = (bf16[1536,384]{1,0:T(8,128)(2,1)S(1)}, bf16[1536,384]{1,0:T(8,128)(2,1)}, u32[]{:S(2)}) copy-start(bf16[1536,384]{1,0:T(8,128)(2,1)} %all-gather.23.cloned.1.call-done.right) | copy-start | bytes 3538948
  672.6 368.3 %all-gather.33.cloned.1.call-start = ((), (), s32[]{:S(2)}) async-start(), calls=%async_computation.13 | async-start | bytes 5308416 | tf_op jit(solution)/shard_map/all_gather | solution.py:831
  729.9 351.7 %all-gather.31.cloned.1.call-start = ((), (), s32[]{:S(2)}) async-start(), calls=%async_computation.12 | async-start | bytes 5308416 | tf_op jit(solution)/shard_map/all_gather | solution.py:831
  730.7 398.1 %all-gather.45.cloned.1.call-start = ((), (), s32[]{:S(2)}) async-start(), calls=%async_computation.23 | async-start | bytes 7077888 | tf_op jit(solution)/shard_map/all_gather | solution.py:831
  792.5 383.6 %all-gather.43.cloned.1.call-start = ((), (), s32[]{:S(2)}) async-start(), calls=%async_computation.22 | async-start | bytes 7077888 | tf_op jit(solution)/shard_map/all_gather | solution.py:831
  862.8 68.9 %copy-start.31 = (f32[1,1536]{1,0:T(1,128)S(1)}, f32[1,1536]{1,0:T(1,128)}, u32[]{:S(2)}) copy-start(f32[1,1536]{1,0:T(1,128)} %copy-done.30) | copy-start | bytes 18436
  (89 other events, 893.7 us)
Sparse Core Ops, SparseCore 0:
  16.6 32.9 all-gather.22
  51.8 100.8 all-gather.24
  154.8 44.9 all-gather.34
  201.2 36.2 all-gather.26
  238.9 62.6 all-gather.28
  303.1 35.6 all-gather.36
  537.5 30.1 reduce-scatter.6
  570.6 27.9 reduce-scatter.8
  601.5 34.0 reduce-scatter.16
  638.3 34.2 reduce-scatter.14
  675.0 54.8 all-reduce.2
  732.7 59.7 reduce-scatter.12
  795.4 60.3 reduce-scatter.10
  857.5 38.4 all-gather.38
  897.7 34.5 all-gather.40
  934.0 32.3 all-gather.48
  968.1 32.1 all-gather.46
  1002.1 38.7 all-gather.32
  1042.8 38.7 all-gather.30
  1083.3 45.3 all-gather.44
  1130.7 45.3 all-gather.42
